TPU v7x, 32 devices: a 4x4x1 block of a 4x4x8 slice. The times are simulated.
32 devices in a mesh: dp: 1 (over z), fsdp: 4 (over y), sp: 8 (over x, core).
Axes of the slice: x: 4, y: 4, z: 1, core: 2. Of those that a mesh axis runs over, the one named last changes fastest.
The devices are a block of a 4x4x8 slice.
Arguments:
- x_in: bfloat16 [48, 1024, 2048], P(('dp', 'fsdp'), 'sp')
- norm_attn: bfloat16 [2048], P('fsdp')
- w_query: bfloat16 [2048, 2048], P('fsdp')
- w_key: bfloat16 [2048, 2048], P('fsdp')
- w_value: bfloat16 [2048, 2048], P('fsdp')
- w_out: bfloat16 [2048, 2048], P('fsdp')
- norm_mlp: bfloat16 [2048], P('fsdp')
- w_gate: bfloat16 [2048, 5504], P('fsdp')
- w_up: bfloat16 [2048, 5504], P('fsdp')
- w_down: bfloat16 [5504, 2048], P('fsdp')
Outputs:
- output: bfloat16 [48, 1024, 2048], P(('dp', 'fsdp'), 'sp')
All inputs are finite; a program needn't handle non-finite values.
Results may differ from a plain program's by a relative error of at most 0.011195.
Values are sent between devices in bfloat16 or wider.
A program may use at most 768 MiB of HBM per device.

v0:
```python
import math
import functools
import jax
import jax.numpy as jnp
from jax import lax
from jax.sharding import PartitionSpec as P

HEAD_DIM = 128
NORM_EPS = 1e-5
ROPE_THETA = 5e7
MASK_VALUE = -1e30


def rms_norm(hidden, gain):
    hid_f32 = hidden.astype(jnp.float32)
    inv_rms = lax.rsqrt(jnp.mean(hid_f32 * hid_f32, axis=-1, keepdims=True) + NORM_EPS)
    return (hid_f32 * inv_rms * gain.astype(jnp.float32)).astype(jnp.bfloat16)


def apply_rope(proj, angles):
    half_dim = proj.shape[-1] // 2
    lower_half = proj[..., :half_dim]
    upper_half = proj[..., half_dim:]
    cos_tab = jnp.cos(angles)[..., None, :]
    sin_tab = jnp.sin(angles)[..., None, :]
    return jnp.concatenate([lower_half * cos_tab - upper_half * sin_tab, upper_half * cos_tab + lower_half * sin_tab], axis=-1)


def rope_angles(token_pos):
    inv_freq = jnp.exp(jnp.arange(HEAD_DIM // 2, dtype=jnp.float32) * (-2.0 * math.log(ROPE_THETA) / HEAD_DIM))
    return token_pos.astype(jnp.float32)[:, None] * inv_freq[None, :]


def gather_weight(weight_shard):
    return lax.all_gather(weight_shard, 'fsdp', axis=0, tiled=True)


def local_layer(x_loc, norm_attn, w_query, w_key, w_value, w_out, norm_mlp, w_gate, w_up, w_down, num_shards):
    num_rows, shard_len, model_dim = x_loc.shape
    head_shape = (num_rows, shard_len, model_dim // HEAD_DIM, HEAD_DIM)
    pos_loc = jnp.arange(shard_len, dtype=jnp.int32) * num_shards + lax.axis_index('sp')
    seq_idx = jnp.arange(num_shards * shard_len, dtype=jnp.int32)
    pos_all = (seq_idx % shard_len) * num_shards + seq_idx // shard_len
    angles = rope_angles(pos_loc)
    normed = rms_norm(x_loc, gather_weight(norm_attn))
    query_rot = apply_rope(jnp.dot(normed, gather_weight(w_query), preferred_element_type=jnp.float32).reshape(head_shape), angles).astype(jnp.bfloat16)
    key_rot = apply_rope(jnp.dot(normed, gather_weight(w_key), preferred_element_type=jnp.float32).reshape(head_shape), angles).astype(jnp.bfloat16)
    value_loc = jnp.dot(normed, gather_weight(w_value), preferred_element_type=jnp.float32).astype(jnp.bfloat16).reshape(head_shape)
    key_all = lax.all_gather(key_rot, 'sp', axis=1, tiled=True)
    value_all = lax.all_gather(value_loc, 'sp', axis=1, tiled=True)
    scores = jnp.einsum('bqhd,bkhd->bhqk', query_rot, key_all, preferred_element_type=jnp.float32) * HEAD_DIM ** -0.5
    allowed = pos_all[None, None, None, :] <= pos_loc[None, None, :, None]
    attn_prob = jax.nn.softmax(jnp.where(allowed, scores, MASK_VALUE), axis=-1).astype(jnp.bfloat16)
    attn_mix = jnp.einsum('bhqk,bkhd->bqhd', attn_prob, value_all, preferred_element_type=jnp.float32).astype(jnp.bfloat16).reshape(num_rows, shard_len, model_dim)
    resid = (x_loc.astype(jnp.float32) + jnp.dot(attn_mix, gather_weight(w_out), preferred_element_type=jnp.float32)).astype(jnp.bfloat16)
    normed_mlp = rms_norm(resid, gather_weight(norm_mlp))
    gate_act = jax.nn.silu(jnp.dot(normed_mlp, gather_weight(w_gate), preferred_element_type=jnp.float32))
    up_proj = jnp.dot(normed_mlp, gather_weight(w_up), preferred_element_type=jnp.float32)
    hidden_mlp = (gate_act * up_proj).astype(jnp.bfloat16)
    return (resid.astype(jnp.float32) + jnp.dot(hidden_mlp, gather_weight(w_down), preferred_element_type=jnp.float32)).astype(jnp.bfloat16)


def solution(mesh):
    row_spec = P(('dp', 'fsdp'), 'sp', None)
    weight_spec = P('fsdp', None)
    gain_spec = P('fsdp')
    in_specs = (row_spec, gain_spec, weight_spec, weight_spec, weight_spec, weight_spec, gain_spec, weight_spec, weight_spec, weight_spec)
    layer_fn = functools.partial(local_layer, num_shards=mesh.shape['sp'])
    return jax.shard_map(layer_fn, mesh=mesh, in_specs=in_specs, out_specs=row_spec, check_vma=False)
```

profile of v0, /device:TPU:97, one launch (start us, length us, event | category | flops | bytes accessed | tf_op | source)
XLA Modules:
  0.0 1500.6 jit_solution(8422206807664919228)
XLA Ops:
  6.6 0.7 all-gather.16.cloned.1.call-update
  7.4 0.7 all-gather.18.cloned.1.call-update
  8.2 0.7 all-gather.12.cloned.1.call-update
  9.7 11.6 all-gather
  21.3 4.1 fusion.12
  25.7 67.8 %all-gather.16.cloned.1.call-done = bf16[2048,2048]{1,0:T(8,128)(2,1)} async-done(((bf16[512,2048]{1,0:T(8,128)(2,1)}), bf16[2048,2048]{1,0:T(8,128)(2,1)}) %all-gather.16.cloned.1.call-update) | async-done | bytes 8388624 | tf_op jit(solution)/shard_map/all_gather | solution.py:35
  93.4 19.1 %fusion.24 = f32[12,128,2048]{2,1,0:T(8,128)} fusion(bf16[2048,2048]{1,0:T(8,128)(2,1)} %all-gather.16.cloned.1.call-done, bf16[12,128,2048]{2,1,0:T(8,128)(2,1)} %param.10, f32[2048]{0:T(1024)S(1)} %bitcast.53, f32[12,128]{1,0:T(8,128)S(1)} %add_rsqrt_fusion.1), kind=kOutput, calls=%fused_computation.38 | convolution fusion | flops 12897484800 | bytes 27277312 | tf_op jit(solution)/shard_map/dot_general | solution.py:46
  112.6 12.2 copy.29
  124.7 52.0 %all-gather.18.cloned.1.call-done = bf16[2048,2048]{1,0:T(8,128)(2,1)} async-done(((bf16[512,2048]{1,0:T(8,128)(2,1)}), bf16[2048,2048]{1,0:T(8,128)(2,1)}) %all-gather.18.cloned.1.call-update) | async-done | bytes 8388624 | tf_op jit(solution)/shard_map/all_gather | solution.py:35
  176.8 19.4 %fusion.22 = f32[12,128,2048]{2,1,0:T(8,128)} fusion(bf16[2048,2048]{1,0:T(8,128)(2,1)} %all-gather.18.cloned.1.call-done, bf16[12,128,2048]{2,1,0:T(8,128)(2,1)} %param.10, f32[2048]{0:T(1024)S(1)} %bitcast.54, f32[12,128]{1,0:T(8,128)S(1)} %add_rsqrt_fusion.1), kind=kOutput, calls=%fused_computation.36 | convolution fusion | flops 12897484800 | bytes 27277312 | tf_op jit(solution)/shard_map/dot_general | solution.py:47
  196.2 12.1 copy.30
  208.3 34.8 %fusion.59 = (f32[12,128,16,64]{3,2,1,0:T(8,128)}, f32[12,128,16,64]{3,2,1,0:T(8,128)}, f32[12,128,16,64]{3,2,1,0:T(8,128)}, f32[12,128,16,64]{3,2,1,0:T(8,128)}) fusion(f32[12,128,16,128]{3,2,1,0:T(8,128)} %bitcast.48, f32[12,128,16,128]{3,2,1,0:T(8,128)} %bitcast.49), kind=kLoop, calls=%fused_computation.74 | loop fusion | bytes 50331648 | tf_op jit(solution)/shard_map/slice | solution.py:22
  243.1 36.7 %subtract_convert_fusion.1 = (bf16[12,128,16,64]{3,1,2,0:T(8,128)(2,1)}, bf16[12,128,16,64]{3,1,2,0:T(8,128)(2,1)}, bf16[12,128,16,64]{3,1,2,0:T(8,128)(2,1)}, bf16[12,128,16,64]{3,1,2,0:T(8,128)(2,1)}) fusion(f32[12,128,16,64]{3,2,1,0:T(8,128)} %get-tuple-element.10, f32[12,128,16,64]{3,2,1,0:T(8,128)} %get-tuple-element.9, ...), kind=kLoop, calls=%fused_computation.33 | loop fusion | flops 25165824 | bytes 37814272 | tf_op jit(solution)/shard_map/convert.2
  279.8 9.7 pad_maximum_fusion
  289.6 19.2 %fusion.36 = bf16[12,128,2048]{2,1,0:T(8,128)(2,1)} fusion(bf16[2048,2048]{1,0:T(8,128)(2,1)} %all-gather.12.cloned.1.call-done, bf16[12,128,2048]{2,1,0:T(8,128)(2,1)} %param.10, f32[2048]{0:T(1024)S(1)} %bitcast.55, f32[12,128]{1,0:T(8,128)S(1)} %add_rsqrt_fusion.1), kind=kOutput, calls=%fused_computation.47 | convolution fusion | flops 12900630528 | bytes 20985856 | tf_op jit(solution)/shard_map/dot_general | solution.py:48
  308.8 8.6 copy.24
  318.1 0.7 all-gather.24.cloned.1.call-update
  319.0 0.7 all-gather.26.cloned.1.call-update
  320.5 10.2 all-gather.1
  331.5 185.2 %all-gather.20.cloned.1.call-done = bf16[12,1024,16,128]{3,1,2,0:T(8,128)(2,1)} async-done(((bf16[12,128,16,128]{3,1,2,0:T(8,128)(2,1)}), bf16[12,1024,16,128]{3,1,2,0:T(8,128)(2,1)}) %all-gather.20.cloned.1.call-update) | async-done | bytes 50331664 | tf_op jit(solution)/shard_map/all_gather | solution.py:49
  516.6 56.2 %fusion.28 = f32[12,16,128,1024]{3,2,1,0:T(8,128)} fusion(bf16[12,1024,16,128]{3,1,2,0:T(8,128)(2,1)} %all-gather.20.cloned.1.call-done, bf16[12,128,16,64]{3,1,2,0:T(8,128)(2,1)} %get-tuple-element.6, bf16[12,128,16,64]{3,1,2,0:T(8,128)(2,1)} %get-tuple-element.5), kind=kOutput, calls=%fused_computation.42 | convolution fusion | flops 6455033856 | bytes 157286400 | tf_op jit(solution)/shard_map/bqhd,bkhd->bhqk/dot_general | solution.py:51
  572.9 99.6 %fusion.61 = (f32[12,16,128]{2,1,0:T(8,128)S(1)}, f32[12,16,128,1024]{3,2,1,0:T(8,128)}) fusion(f32[12,16,128,1024]{3,2,1,0:T(8,128)} %fusion.28, pred[128,1024]{1,0:T(8,128)(4,1)S(1)} %broadcast_compare_fusion), kind=kOutput, calls=%fused_computation.76 | output fusion | flops 150995968 | bytes 201555968 | tf_op jit(solution)/shard_map/sub | solution.py:53
  672.4 79.7 %all-gather.14.cloned.1.call-done = bf16[12,1024,16,128]{1,3,2,0:T(8,128)(2,1)} async-done(((bf16[12,128,16,128]{1,3,2,0:T(8,128)(2,1)}), bf16[12,1024,16,128]{1,3,2,0:T(8,128)(2,1)}) %all-gather.14.cloned.1.call-update) | async-done | bytes 50331664 | tf_op jit(solution)/shard_map/all_gather | solution.py:50
  752.2 49.1 %fusion.41 = bf16[12,16,128,128]{3,2,1,0:T(8,128)(2,1)} fusion(bf16[12,1024,16,128]{1,3,2,0:T(8,128)(2,1)} %all-gather.14.cloned.1.call-done, f32[12,16,128,1024]{3,2,1,0:T(8,128)} %get-tuple-element.18, f32[12,16,128]{2,1,0:T(8,128)S(1)} %get-tuple-element.17), kind=kOutput, calls=%fused_computation.48 | convolution fusion | flops 6495928320 | bytes 157384704 | tf_op jit(solution)/shard_map/bhqk,bkhd->bqhd/dot_general | solution.py:54
  801.3 33.5 %all-gather.22.cloned.1.call-done = bf16[2048,2048]{1,0:T(8,128)(2,1)} async-done(((bf16[512,2048]{1,0:T(8,128)(2,1)}), bf16[2048,2048]{1,0:T(8,128)(2,1)}) %all-gather.22.cloned.1.call-update) | async-done | bytes 8388624 | tf_op jit(solution)/shard_map/all_gather | solution.py:35
  834.7 21.3 %fusion.16 = (f32[12,128]{1,0:T(8,128)S(1)}, bf16[12,128,2048]{2,1,0:T(8,128)(2,1)}) fusion(bf16[12,128,2048]{1,2,0:T(8,128)(2,1)} %bitcast.58, bf16[2048,2048]{1,0:T(8,128)(2,1)} %all-gather.22.cloned.1.call-done, bf16[12,128,2048]{2,1,0:T(8,128)(2,1)} %param.10), kind=kOutput, calls=%fused_computation.26 | convolution fusion | flops 12903774208 | bytes 27269120 | tf_op jit(solution)/shard_map/dot_general | solution.py:55
  856.1 181.9 %all-gather.24.cloned.1.call-done = bf16[2048,5504]{1,0:T(8,128)(2,1)} async-done(((bf16[512,5504]{1,0:T(8,128)(2,1)}), bf16[2048,5504]{1,0:T(8,128)(2,1)}) %all-gather.24.cloned.1.call-update) | async-done | bytes 22544400 | tf_op jit(solution)/shard_map/all_gather | solution.py:35
  1038.0 45.2 %fusion.10 = f32[12,128,5504]{2,1,0:T(8,128)} fusion(bf16[2048,5504]{1,0:T(8,128)(2,1)} %all-gather.24.cloned.1.call-done, bf16[12,128,2048]{2,1,0:T(8,128)(2,1)} %get-tuple-element.20, f32[2048]{0:T(1024)S(1)} %bitcast.56, f32[12,128]{1,0:T(8,128)S(1)} %add_rsqrt_fusion), kind=kOutput, calls=%fused_computation.14 | convolution fusion | flops 34640756736 | bytes 62666752 | tf_op jit(solution)/shard_map/dot_general | solution.py:57
  1083.2 157.5 %all-gather.26.cloned.1.call-done = bf16[2048,5504]{1,0:T(8,128)(2,1)} async-done(((bf16[512,5504]{1,0:T(8,128)(2,1)}), bf16[2048,5504]{1,0:T(8,128)(2,1)}) %all-gather.26.cloned.1.call-update) | async-done | bytes 22544400 | tf_op jit(solution)/shard_map/all_gather | solution.py:35
  1240.7 45.3 %fusion.8 = f32[12,128,5504]{2,1,0:T(8,128)} fusion(bf16[2048,5504]{1,0:T(8,128)(2,1)} %all-gather.26.cloned.1.call-done, bf16[12,128,2048]{2,1,0:T(8,128)(2,1)} %get-tuple-element.20, f32[2048]{0:T(1024)S(1)} %bitcast.57, f32[12,128]{1,0:T(8,128)S(1)} %add_rsqrt_fusion), kind=kOutput, calls=%fused_computation.12 | convolution fusion | flops 34640756736 | bytes 62666752 | tf_op jit(solution)/shard_map/dot_general | solution.py:58
  1286.0 157.5 %all-gather.28.cloned.1.call-done = bf16[5504,2048]{1,0:T(8,128)(2,1)} async-done(((bf16[1376,2048]{1,0:T(8,128)(2,1)}), bf16[5504,2048]{1,0:T(8,128)(2,1)}) %all-gather.28.cloned.1.call-update) | async-done | bytes 22544400 | tf_op jit(solution)/shard_map/all_gather | solution.py:35
  1443.5 50.1 %fusion.19 = bf16[12,128,2048]{2,1,0:T(8,128)(2,1)} fusion(bf16[12,128,2048]{2,1,0:T(8,128)(2,1)} %get-tuple-element.20, bf16[5504,2048]{1,0:T(8,128)(2,1)} %all-gather.28.cloned.1.call-done, f32[12,128,5504]{2,1,0:T(8,128)} %fusion.8, f32[12,128,5504]{2,1,0:T(8,128)} %fusion.10), kind=kOutput, calls=%fused_computation.29 | convolution fusion | flops 34688335872 | bytes 102760448 | tf_op jit(solution)/shard_map/dot_general | solution.py:60
  (30 shorter events, 3.7 us)
Async XLA Ops:
  6.5 86.9 %all-gather.16.cloned.1.call-start = ((), (), s32[]{:S(2)}) async-start(), calls=%async_computation.2 | async-start | bytes 10485760 | tf_op jit(solution)/shard_map/all_gather | solution.py:35
  7.3 169.4 %all-gather.18.cloned.1.call-start = ((), (), s32[]{:S(2)}) async-start(), calls=%async_computation.3 | async-start | bytes 10485760 | tf_op jit(solution)/shard_map/all_gather | solution.py:35
  8.1 281.5 %all-gather.12.cloned.1.call-start = ((), (), s32[]{:S(2)}) async-start(), calls=%async_computation | async-start | bytes 10485760 | tf_op jit(solution)/shard_map/all_gather | solution.py:35
  8.9 507.7 %all-gather.20.cloned.1.call-start = ((), (), s32[]{:S(2)}) async-start(), calls=%async_computation.4 | async-start | bytes 56623104 | tf_op jit(solution)/shard_map/all_gather | solution.py:49
  289.5 462.7 %all-gather.14.cloned.1.call-start = ((), (), s32[]{:S(2)}) async-start(), calls=%async_computation.1 | async-start | bytes 56623104 | tf_op jit(solution)/shard_map/all_gather | solution.py:50
  317.4 3.1 copy-start.1
  317.4 517.3 %all-gather.22.cloned.1.call-start = ((), (), s32[]{:S(2)}) async-start(), calls=%async_computation.5 | async-start | bytes 10485760 | tf_op jit(solution)/shard_map/all_gather | solution.py:35
  318.1 719.9 %all-gather.24.cloned.1.call-start = ((), (), s32[]{:S(2)}) async-start(), calls=%async_computation.6 | async-start | bytes 28180480 | tf_op jit(solution)/shard_map/all_gather | solution.py:35
  318.9 921.9 %all-gather.26.cloned.1.call-start = ((), (), s32[]{:S(2)}) async-start(), calls=%async_computation.7 | async-start | bytes 28180480 | tf_op jit(solution)/shard_map/all_gather | solution.py:35
  319.7 1123.8 %all-gather.28.cloned.1.call-start = ((), (), s32[]{:S(2)}) async-start(), calls=%async_computation.8 | async-start | bytes 28180480 | tf_op jit(solution)/shard_map/all_gather | solution.py:35
  834.7 203.2 %copy-start = (f32[4,1,512]{2,1,0:T(1,128)S(1)}, f32[4,1,512]{2,1,0:T(1,128)}, u32[]{:S(2)}) copy-start(f32[4,1,512]{2,1,0:T(1,128)} %convert_element_type.65) | copy-start | bytes 24580
Sparse Core Ops, SparseCore 0:
  8.9 84.4 all-gather.15
  95.0 81.6 all-gather.17
  178.3 81.6 all-gather.11
  289.6 226.9 all-gather.19
  518.1 234.0 all-gather.13
  753.6 81.0 all-gather.21
  836.3 201.6 all-gather.23
  1039.6 201.1 all-gather.25
  1242.3 201.1 all-gather.27
where the time goes:
time: 1510 us; the launch traced here: 1500 us
  waiting for transfers between devices  920 us (61%)
  matrix products  325 us (22%)
  other arithmetic  151 us (10%)
  local copies, waits for them, and re-layouts  68.4 us (5%)
  blocking collectives  21.8 us (1%)
    all_gather x7, waiting for transfers between devices, gather_weight(): return lax.all_gather(weight_shard, 'fsdp', axis=0, tiled=True)  650 us
    all_gather x1, waiting for transfers between devices, local_layer(): key_all = lax.all_gather(key_rot, 'sp', axis=1, tiled=True)  185 us
    sub x1, other arithmetic, local_layer(): jax.nn.softmax(jnp.where(allowed, scores, MASK_VALUE), axis=-1)  99.6 us
    all_gather x1, waiting for transfers between devices, local_layer(): value_all = lax.all_gather(value_loc, 'sp', axis=1, tiled=True)  79.7 us
    dot_general x1, matrix products, local_layer(): jnp.einsum('bqhd,bkhd->bhqk', query_rot, key_all, preferred_element_type=...  56.2 us
    dot_general x1, matrix products, local_layer(): jnp.dot(hidden_mlp, gather_weight(w_down), preferred_element_type=jnp.flo...  50.1 us
    dot_general x1, matrix products, local_layer(): jnp.einsum('bhqk,bkhd->bqhd', attn_prob, value_all, preferred_element_typ...  49.1 us
    dot_general x1, matrix products, local_layer(): jnp.dot(normed_mlp, gather_weight(w_up), preferred_element_type=jnp.float32)  45.3 us
  transfers between devices with their start and end apart: 9, of which 8 were waited for; matrix products, arithmetic and copies ran while one was open for 33% of the time, Pallas kernels for 0%

commit v1 on v0

v1 whole, which is shorter than its diff:
```python
import functools
import math

import jax
import jax.numpy as jnp
from jax import lax
from jax.experimental import pallas as pl
from jax.experimental.pallas import tpu as pltpu
from jax.sharding import PartitionSpec as P

HEAD = 128
EPS = 1e-5
THETA = 5e7
MASKED = -1e30
CB = 256
SUB = 16
MESH = pl.DeviceIdType.MESH
F32 = jnp.float32
BF16 = jnp.bfloat16


def kernel(cfg, x_hbm, gin, cos_t, sin_t, mask_t, wq, wk, wv, wo, wg, wu, wd, out, bq, bo, bg, bd, H, B, U, OST, QS, KS, VS, W, FA, FO, G, XC, YC, XN,
           rsem, ssem, gsem, gssem, asem, assem, fasem, fassem, shsem, osem, ossem, fosem, fossem, wsem, xcsem, ycsem, xnsem):
    nf, nx, D, F, ROWS, NRB, NS = cfg
    RC = ROWS // nx
    NHG = D // CB
    q4 = NHG // 2
    y = lax.axis_index("fsdp")
    s = lax.axis_index("sp")
    x = s // 2
    c = s % 2
    par = x % 2

    def dev(xx, cc):
        return {"sp": 2 * ((xx + nx) % nx) + cc}

    def ydev(d):
        return {"fsdp": (y + d + nf) % nf}

    sib = {"sp": 2 * x + 1 - c}

    def rcopy(src, dst, ssem_, rsem_, to):
        pltpu.make_async_remote_copy(src_ref=src, dst_ref=dst, send_sem=ssem_, recv_sem=rsem_, device_id=to, device_id_type=MESH).start()

    def wait(view, sem):
        pltpu.make_async_copy(view, view, sem).wait()

    NGU = pl.cdiv(F, CB)
    RD, RF = D // nf, F // nf
    classes = []
    base = 0
    for ws, buf, R, n, two, look in (
        ((wq, wk, wv), bq, RD, NHG, False, 2),
        ((wo,), bo, RD, NHG, False, 3),
        ((wg, wu), bg, RD, NGU, True, 3),
        ((wd,), bd, RF, NHG, True, 3),
    ):
        nr = R // 4 if two else R // 2
        ra = ((nr // 8 + 1) // 2) * 8
        p0 = pl.multiple_of((2 * par + c) * nr if two else c * nr, 8)
        q0 = pl.multiple_of((2 * (1 - par) + c) * nr, 8) if two else None
        ncols = ws[0].shape[1]
        classes.append(dict(ws=ws, buf=buf, R=R, n=n, base=base, two=two, look=look, nr=nr, ra=ra, p0=p0, q0=q0, ncols=ncols, ci=len(classes)))
        base += n
    NSTEP = base
    HGc, Oc, GUc, DNc = classes

    def col0(k, j):
        return pl.multiple_of(jnp.minimum(j * CB, k["ncols"] - CB), 128)

    def each(it, shift, f):
        for k in classes:
            j = it + shift(k) - k["base"]

            @pl.when((j >= 0) & (j < k["n"]))
            def _(k=k, j=j):
                f(k, j)

    def s1_send(k, j):
        rows = pl.ds(k["p0"], k["nr"])
        cols = pl.ds(col0(k, j), CB)
        for wi, w in enumerate(k["ws"]):
            src = w.at[rows, cols]
            rcopy(src, k["buf"].at[j, wi, 2, rows], ssem.at[k["ci"], 0], rsem.at[k["base"] + j, 0], ydev(1))
            rcopy(src, k["buf"].at[j, wi, 0, rows], ssem.at[k["ci"], 0], rsem.at[k["base"] + j, 0], ydev(-1))

    def s1_done(k, j):
        b, ra, nr = k["buf"], k["ra"], k["nr"]
        wait(b.at[j, :, pl.ds(0, 2), pl.ds(k["p0"], nr)], rsem.at[k["base"] + j, 0])
        A = pl.ds(k["p0"], ra)
        Z = pl.ds(pl.multiple_of(k["p0"] + ra, 8), nr - ra)
        rcopy(b.at[j, :, 2, A], b.at[j, :, 1, A], ssem.at[k["ci"], 1], rsem.at[k["base"] + j, 1], ydev(1))
        rcopy(b.at[j, :, 0, Z], b.at[j, :, 1, Z], ssem.at[k["ci"], 1], rsem.at[k["base"] + j, 1], ydev(-1))

    def s2_done(k, j):
        b, ra, nr = k["buf"], k["ra"], k["nr"]
        wait(b.at[j, :, 1, pl.ds(k["p0"], nr)], rsem.at[k["base"] + j, 1])
        rows = pl.ds(k["p0"], nr)
        if k["two"]:
            A = pl.ds(k["p0"], ra)
            Z = pl.ds(pl.multiple_of(k["p0"] + ra, 8), nr - ra)
            rcopy(b.at[j, :, :, A], b.at[j, :, :, A], ssem.at[k["ci"], 2], rsem.at[k["base"] + j, 2], dev(x + 1, c))
            rcopy(b.at[j, :, :, Z], b.at[j, :, :, Z], ssem.at[k["ci"], 2], rsem.at[k["base"] + j, 2], dev(x - 1, c))
        rcopy(b.at[j, :, :, rows], b.at[j, :, :, rows], ssem.at[k["ci"], 3], rsem.at[k["base"] + j, 3], sib)

    def x_done(k, j):
        if k["two"]:
            b = k["buf"]
            rows = pl.ds(k["q0"], k["nr"])
            wait(b.at[j, :, :, rows], rsem.at[k["base"] + j, 2])
            rcopy(b.at[j, :, :, rows], b.at[j, :, :, rows], ssem.at[k["ci"], 3], rsem.at[k["base"] + j, 3], sib)

    def d_wait(k, j):
        wait(k["buf"].at[j, :, :, pl.ds(0, k["R"] // 2)], rsem.at[k["base"] + j, 3])

    def w_load(k, j, slot):
        R = k["R"]
        for wi, w in enumerate(k["ws"]):
            o = wi * nf * R
            pltpu.make_async_copy(w.at[:, pl.ds(col0(k, j), CB)], W.at[slot, pl.ds(pl.multiple_of(o + y * R, 8), R)], wsem.at[slot]).start()
            for r in range(1, nf):
                yy = (y + r) % nf
                pltpu.make_async_copy(k["buf"].at[j, wi, r - 1], W.at[slot, pl.ds(pl.multiple_of(o + yy * R, 8), R)], wsem.at[slot]).start()

    def w_wait(k, slot):
        wait(W.at[slot, pl.ds(0, len(k["ws"]) * nf * k["R"])], wsem.at[slot])

    bar = pltpu.get_barrier_semaphore()
    peers = [ydev(d) for d in range(1, nf)] + [dev(x + 1, 0), dev(x + 1, 1), dev(x - 1, 0), dev(x - 1, 1), sib]
    for p in peers:
        pl.semaphore_signal(bar, inc=1, device_id=p, device_id_type=MESH)
    pl.semaphore_wait(bar, len(peers))

    gcols = pl.ds(pl.multiple_of(y * RD, 128), RD)
    for d in range(1, nf):
        rcopy(gin, G.at[:, gcols], gssem, gsem, ydev(d))
    for i in range(HGc["look"]):
        s1_send(HGc, i)
    G[:, gcols] = gin[...]

    def xn_load(n):
        r = RC * ((x + nx + 2 - n % nx) % nx) + n // nx
        return pltpu.make_async_copy(x_hbm.at[r], XN.at[n % 2], xnsem.at[n % 2])

    xn_load(0).start()
    wait(G.at[:, pl.ds(0, (nf - 1) * RD)], gsem)

    def av(k, src):
        return U.at[pl.ds(0, NRB), src, :, pl.ds(pl.multiple_of(k * D, 128), D)]

    def rms(src, dst, grow, extra=None):
        g = G[pl.ds(grow, 1), :]

        def one(i, carry):
            h = src[i].astype(F32)
            inv = lax.rsqrt(jnp.mean(h * h, axis=-1, keepdims=True) + EPS)
            a = (h * inv * g).astype(BF16)
            dst[i] = a
            return carry

        lax.fori_loop(0, NRB, one, 0, unroll=2)

    def norm_row(n, carry):
        k = n // nx
        d = (nx + 2 - n % nx) % nx
        xd = (x + d) % nx
        r = RC * xd + k
        xn_load(n).wait()

        @pl.when(n + 1 < ROWS)
        def _():
            xn_load(n + 1).start()

        rms(XN.at[n % 2], H.at[r], 0)
        src = H.at[r]

        @pl.when((d == 1) | (d == nx - 1))
        def _():
            @pl.when(k < 2)
            def _():
                rcopy(src, av(0, s), assem, asem.at[0], dev(xd, k))

            @pl.when(k == 2)
            def _():
                rcopy(src, av(1, s), assem, asem.at[1], dev(xd, c))

        @pl.when(d == 2)
        def _():
            rcopy(src, FA.at[k], assem, fasem.at[k], dev(x + 1 - 2 * c, c))

        @pl.when((d == 0) & (k == 1 - c))
        def _():
            rcopy(src, av(0, s), assem, asem.at[0], sib)

        @pl.when((d == 0) & (k == 2))
        def _():
            rcopy(src, av(1, s), assem, asem.at[2], sib)

        @pl.when((d == 0) & ((k == c) | (k == 2)))
        def _():
            kk = k // 2
            U[pl.ds(0, NRB), s, :, pl.ds(pl.multiple_of(kk * D, 128), D)] = H[r]

        return carry

    lax.fori_loop(0, ROWS, norm_row, 0)

    def unit(n):
        m = n - q4
        odd = (n >= q4) & (m % 2 == 1)
        kk = jnp.where(odd, 1, 0)
        hg = jnp.where(odd, 2 * (m // 2) + c, jnp.where(n < q4, n, q4 + m // 2))
        return kk, hg

    def unit_row(kk, xx):
        return RC * ((xx + nx) % nx) + jnp.where(kk == 1, 2, c)

    def unit_load(n):
        kk, hg = unit(n)

        @pl.when(kk == 0)
        def _():
            d_wait(HGc, hg)

        w_load(HGc, hg, n % 2)

    QT = 2 * NS * SUB
    NQT = NRB // 2
    scale2 = (HEAD ** -0.5) * math.log2(math.e)

    def unit_run(n, carry):
        kk, hg = unit(n)
        slot = n % 2
        hcols = pl.ds(pl.multiple_of(hg * CB, CB), CB)

        @pl.when(n == 0)
        def _():
            wait(U.at[pl.ds(0, NRB - 1), :, :, pl.ds(0, D)], asem.at[0])

        @pl.when(n == q4 + 1)
        def _():
            wait(U.at[pl.ds(0, NRB // 2), :, :, pl.ds(0, D)], asem.at[2])

        w_wait(HGc, slot)

        def proj(t, cr):
            rows = pl.ds(pl.multiple_of(t * QT, QT), QT)
            a = U[pl.ds(t * 2, 2), :, :, pl.ds(pl.multiple_of(kk * D, 128), D)].reshape(QT, D)
            cs = cos_t[rows, :]
            sn = sin_t[rows, :]
            for wi, dst in enumerate((QS, KS)):
                p = jnp.dot(a, W[slot, pl.ds(wi * D, D), :], preferred_element_type=F32)
                for h in range(CB // HEAD):
                    ph = p[:, h * HEAD:(h + 1) * HEAD]
                    dst[rows, h * HEAD:(h + 1) * HEAD] = (ph * cs + pltpu.roll(ph, HEAD // 2, 1) * sn).astype(BF16)
            VS[rows, :] = jnp.dot(a, W[slot, pl.ds(2 * D, D), :], preferred_element_type=F32).astype(BF16)
            return cr

        lax.fori_loop(0, NQT, proj, 0)

        @pl.when(n + 1 < 3 * q4)
        def _():
            unit_load(n + 1)

        def head(h, cr):
            hc = pl.ds(pl.multiple_of(h * HEAD, HEAD), HEAD)
            for t in range(NQT):
                kl = (t + 1) * QT
                sc = lax.dot_general(QS[pl.ds(t * QT, QT), hc], KS[pl.ds(0, kl), hc], (((1,), (1,)), ((), ())), preferred_element_type=F32)
                diag = jnp.where(mask_t[...] > 0.0, sc[:, t * QT:], MASKED)
                if t:
                    sc = jnp.concatenate([sc[:, :t * QT], diag], axis=1)
                else:
                    sc = diag
                mx = jnp.max(sc, axis=-1, keepdims=True)
                p = jnp.exp2((sc - mx) * scale2)
                ls = jnp.sum(p, axis=-1, keepdims=True)
                o = jnp.dot(p.astype(BF16), VS[pl.ds(0, kl), hc], preferred_element_type=F32)
                o = (o * (1.0 / ls)).astype(BF16)
                OST[n, pl.ds(2 * t, 2), :, :, hc] = o.reshape(2, NS, SUB, HEAD)
            return cr

        lax.fori_loop(0, CB // HEAD, head, 0)

        row = unit_row(kk, x)
        B[row, :, :, hcols] = OST[n, :, s]
        rcopy(OST.at[n, :, 2 * x + 1 - c], B.at[row, :, :, hcols], ossem.at[n], osem.at[row], sib)
        far = (x + 2) % nx
        rcopy(OST.at[n, :, pl.ds(2 * far, 2)], FO.at[n], ossem.at[n], fosem.at[n], dev(x + 1 - 2 * c, c))
        for dx in (1, nx - 1):
            for cc in range(2):
                xd = (x + dx) % nx
                rcopy(OST.at[n, :, 2 * xd + cc], B.at[row, :, :, hcols], ossem.at[n], osem.at[row], dev(xd, cc))
        return carry

    def unit_forward(n, carry):
        kk, hg = unit(n)
        wait(FO.at[n], fosem.at[n])
        row = unit_row(kk, x - 1 + 2 * c)
        for cc in range(2):
            rcopy(FO.at[n, :, cc], B.at[row, :, :, pl.ds(pl.multiple_of(hg * CB, CB), CB)], fossem.at[n], osem.at[row], dev(x + 1 - 2 * c, cc))
        return carry

    def ustart(it):
        late = jnp.minimum(q4 + 2 * (it - q4 - 2), 3 * q4)
        early = jnp.where(it <= 3, 0, jnp.clip(it - 2, 0, q4)) if q4 > 2 else jnp.clip(it - 2, 0, q4)
        return jnp.where(it >= q4 + 2, late, early)

    MT = 6
    NMT = ROWS // MT
    TM = MT * NRB * SUB
    NOQ = NHG
    OPI = max(1, NHG // 4)

    def xc_load(j, slot):
        return pltpu.make_async_copy(x_hbm.at[:, :, :, pl.ds(pl.multiple_of(j * CB, CB), CB)], XC.at[slot], xcsem.at[slot])

    def yc_copy(j, slot):
        return pltpu.make_async_copy(YC.at[slot], out.at[:, :, :, pl.ds(pl.multiple_of(j * CB, CB), CB)], ycsem.at[slot])

    def prep(qn):
        for k in (Oc, GUc, DNc):
            j = qn + HGc["n"] - k["base"]

            @pl.when((j >= 0) & (j < k["n"]))
            def _(k=k, j=j):
                d_wait(k, j)
                w_load(k, j, qn % 2)
                if k is Oc:
                    xc_load(j, qn % 2).start()

    def o_step(j):
        slot = j % 2
        w_wait(Oc, slot)
        xc_load(j, slot).wait()
        prep(j + 1)
        cols = pl.ds(pl.multiple_of(j * CB, CB), CB)

        def tile(t, cr):
            rr = pl.ds(t * MT, MT)
            p = jnp.dot(B[rr].reshape(TM, D), W[slot, pl.ds(0, D), :], preferred_element_type=F32)
            h = XC[slot, rr].reshape(TM, CB).astype(F32) + p
            H[rr, :, :, cols] = h.astype(BF16).reshape(MT, NRB, SUB, CB)
            return cr

        lax.fori_loop(0, NMT, tile, 0)

    def gu_step(j):
        qn = Oc["n"] + j
        slot = qn % 2
        w_wait(GUc, slot)
        prep(qn + 1)
        cols = pl.ds(col0(GUc, j), CB)

        def tile(t, cr):
            rr = pl.ds(t * MT, MT)
            b = B[rr].reshape(TM, D)
            g = jnp.dot(b, W[slot, pl.ds(0, D), :], preferred_element_type=F32)
            u = jnp.dot(b, W[slot, pl.ds(D, D), :], preferred_element_type=F32)
            act = g * (1.0 / (1.0 + jnp.exp(-g)))
            U[rr, :, :, cols] = (act * u).astype(BF16).reshape(MT, NRB, SUB, CB)
            return cr

        lax.fori_loop(0, NMT, tile, 0)

    def dn_step(j):
        qn = Oc["n"] + GUc["n"] + j
        slot = qn % 2
        w_wait(DNc, slot)
        prep(qn + 1)
        ys = j % 2

        @pl.when(j >= 2)
        def _():
            yc_copy(j - 2, ys).wait()

        cols = pl.ds(pl.multiple_of(j * CB, CB), CB)

        def tile(t, cr):
            rr = pl.ds(t * MT, MT)
            p = jnp.dot(U[rr].reshape(TM, F), W[slot, pl.ds(0, F), :], preferred_element_type=F32)
            h = H[rr, :, :, cols].reshape(TM, CB).astype(F32) + p
            YC[ys, rr] = h.astype(BF16).reshape(MT, NRB, SUB, CB)
            return cr

        lax.fori_loop(0, NMT, tile, 0)
        yc_copy(j, ys).start()

    LAG = 4
    NIT = NSTEP + LAG
    ogo = GUc["base"]

    def step(it, carry):
        each(it, lambda k: k["look"], s1_send)
        each(it, lambda k: 0, s1_done)
        each(it, lambda k: -1, s2_done)
        each(it, lambda k: -2, x_done)

        @pl.when(it < RC)
        def _():
            wait(FA.at[it], fasem.at[it])
            xs = (x - 1 + 2 * c + nx) % nx
            to = x + 1 - 2 * c

            @pl.when(it < 2)
            def _():
                rcopy(FA.at[it], av(0, 2 * xs + c), fassem, asem.at[0], dev(to, it))

            @pl.when(it == 2)
            def _():
                rcopy(FA.at[it], av(1, 2 * xs + c), fassem, asem.at[1], dev(to, c))

        @pl.when(it == q4 + 1)
        def _():
            wait(U.at[pl.ds(0, nx - 1), :, :, pl.ds(0, D)], asem.at[1])
            for d in range(1, nx):
                src = 2 * ((x + d) % nx) + c
                rcopy(av(1, src), av(1, src), shsem, asem.at[2], sib)

        u0, u1, u2 = ustart(it - 1), ustart(it), ustart(it + 1)
        lax.fori_loop(u0, u1, unit_forward, 0)

        @pl.when((u1 == 0) & (u2 > 0))
        def _():
            unit_load(0)

        lax.fori_loop(u1, u2, unit_run, 0)

        @pl.when(it == ogo)
        def _():
            wait(H.at[pl.ds(0, ROWS - 1)], assem)
            wait(FA, fassem)
            wait(U.at[pl.ds(0, nx - 1), :, :, pl.ds(0, D)], shsem)

            def orow(r, cr):
                k = r % RC

                @pl.when((r // RC != x) | (k == 1 - c))
                def _():
                    wait(B.at[r], osem.at[r])

                @pl.when((r // RC == x) & (k == 2))
                def _():
                    wait(B.at[r, pl.ds(0, NRB // 2)], osem.at[r])

                return cr

            prep(0)
            lax.fori_loop(0, ROWS, orow, 0)

        @pl.when((it >= ogo) & (it < ogo + Oc["n"] // OPI))
        def _():
            def go(i, cr):
                o_step((it - ogo) * OPI + i)
                return cr

            lax.fori_loop(0, OPI, go, 0)

        @pl.when(it == ogo + LAG)
        def _():
            def nrow(r, cr):
                rms(H.at[r], B.at[r], 1)
                return cr

            lax.fori_loop(0, ROWS, nrow, 0)

        @pl.when((it >= GUc["base"] + LAG) & (it < GUc["base"] + LAG + GUc["n"]))
        def _():
            gu_step(it - GUc["base"] - LAG)

        @pl.when((it >= DNc["base"] + LAG) & (it < DNc["base"] + LAG + DNc["n"]))
        def _():
            dn_step(it - DNc["base"] - LAG)

        return carry

    lax.fori_loop(0, NIT, step, 0)

    for j in (DNc["n"] - 2, DNc["n"] - 1):
        yc_copy(j, j % 2).wait()

    def drain(n, cr):
        wait(OST.at[n, :, pl.ds(0, NS - 1)], ossem.at[n])
        wait(FO.at[n], fossem.at[n])
        return cr

    lax.fori_loop(0, 3 * q4, drain, 0)
    wait(G.at[:, pl.ds(0, (nf - 1) * RD)], gssem)
    for k in classes:
        b, nr = k["buf"], k["nr"]
        wait(b.at[:, :, pl.ds(0, 2), pl.ds(0, nr)], ssem.at[k["ci"], 0])
        wait(b.at[:, :, 1, pl.ds(0, nr)], ssem.at[k["ci"], 1])
        if k["two"]:
            wait(b.at[:, :, :, pl.ds(0, nr)], ssem.at[k["ci"], 2])
        wait(b.at[:, :, :, pl.ds(0, k["R"] // 2)], ssem.at[k["ci"], 3])


def local_layer(x, norm_attn, wq, wk, wv, wo, norm_mlp, wg, wu, wd, *, nf, ns):
    rows, tl, D = x.shape
    F = wg.shape[1]
    nx = ns // 2
    nrb = tl // SUB
    nhg = D // CB
    ngu = -(-F // CB)
    units = 3 * nhg // 2
    rd, rf = D // nf, F // nf
    tok = ns * tl

    idx = jnp.arange(tok, dtype=jnp.int32)
    blk, src, low = idx // (ns * SUB), idx % (ns * SUB) // SUB, idx % SUB
    pos = (blk * SUB + low) * ns + src
    inv_freq = jnp.exp(jnp.arange(HEAD // 2, dtype=F32) * (-2.0 * math.log(THETA) / HEAD))
    ang = pos.astype(F32)[:, None] * inv_freq[None, :]
    cs, sn = jnp.cos(ang), jnp.sin(ang)
    cos_t = jnp.concatenate([cs, cs], axis=1)
    sin_t = jnp.concatenate([-sn, sn], axis=1)
    qt = 2 * ns * SUB
    mask_t = (pos[None, :qt] <= pos[:qt, None]).astype(F32)
    gin = jnp.concatenate([norm_attn[None], norm_mlp[None]] + [jnp.zeros((6, rd), norm_attn.dtype)], axis=0).astype(F32)
    x4 = x.reshape(rows, nrb, SUB, D)

    nsteps = nhg * 3 + ngu
    dma = pltpu.SemaphoreType.DMA
    anyspec = pl.BlockSpec(memory_space=pl.ANY)
    vspec = pl.BlockSpec(memory_space=pltpu.VMEM)
    outs = [
        jax.ShapeDtypeStruct((rows, nrb, SUB, D), BF16),
        jax.ShapeDtypeStruct((nhg, 3, nf - 1, rd, CB), BF16),
        jax.ShapeDtypeStruct((nhg, 1, nf - 1, rd, CB), BF16),
        jax.ShapeDtypeStruct((ngu, 2, nf - 1, rd, CB), BF16),
        jax.ShapeDtypeStruct((nhg, 1, nf - 1, rf, CB), BF16),
    ]
    wrows = max(3 * D, F)
    res = pl.pallas_call(
        functools.partial(kernel, (nf, nx, D, F, rows, nrb, ns)),
        out_shape=outs,
        in_specs=[anyspec, vspec, vspec, vspec, vspec] + [anyspec] * 7,
        out_specs=[anyspec] * 5,
        scratch_shapes=[
            pltpu.VMEM((rows, nrb, SUB, D), BF16),
            pltpu.VMEM((rows, nrb, SUB, D), BF16),
            pltpu.VMEM((rows, nrb, SUB, F), BF16),
            pltpu.VMEM((units, nrb, ns, SUB, CB), BF16),
            pltpu.VMEM((tok, CB), BF16),
            pltpu.VMEM((tok, CB), BF16),
            pltpu.VMEM((tok, CB), BF16),
            pltpu.VMEM((2, wrows, CB), BF16),
            pltpu.VMEM((rows // nx, nrb, SUB, D), BF16),
            pltpu.VMEM((units, nrb, 2, SUB, CB), BF16),
            pltpu.VMEM((8, D), F32),
            pltpu.VMEM((2, rows, nrb, SUB, CB), BF16),
            pltpu.VMEM((2, rows, nrb, SUB, CB), BF16),
            pltpu.VMEM((2, nrb, SUB, D), BF16),
            dma((nsteps, 4)),
            dma((4, 4)),
            dma,
            dma,
            dma((3,)),
            dma,
            dma((rows // nx,)),
            dma,
            dma,
            dma((rows,)),
            dma((units,)),
            dma((units,)),
            dma((units,)),
            dma((2,)),
            dma((2,)),
            dma((2,)),
            dma((2,)),
        ],
        compiler_params=pltpu.CompilerParams(collective_id=0, has_side_effects=True, vmem_limit_bytes=66 * 1000 * 1000),
        cost_estimate=pl.CostEstimate(flops=170_000_000_000, bytes_accessed=400_000_000, transcendentals=0),
        name="layer",
    )(x4, gin, cos_t, sin_t, mask_t, wq, wk, wv, wo, wg, wu, wd)
    return res[0].reshape(rows, tl, D)


def solution(mesh):
    row = P(("dp", "fsdp"), "sp", None)
    wspec = P("fsdp", None)
    gspec = P("fsdp")
    fn = functools.partial(local_layer, nf=mesh.shape["fsdp"], ns=mesh.shape["sp"])
    specs = (row, gspec, wspec, wspec, wspec, wspec, gspec, wspec, wspec, wspec)
    return jax.shard_map(fn, mesh=mesh, in_specs=specs, out_specs=row, check_vma=False)
```

time: 1510 us -> 430 us (0.28)
  waiting for transfers between devices: 920 us -> 0 us
  Pallas kernels: 0 us -> 414 us
  matrix products: 325 us -> 0 us
  other arithmetic: 151 us -> 4.7 us
  local copies, waits for them, and re-layouts: 68.4 us -> 8.07 us
  blocking collectives: 21.8 us -> 0 us
    all_gather x9 -> x0, waiting for transfers between devices: 915 us -> none  [the longest x7 650 us: gather_weight(): return lax.all_gather(weight_shard, 'fsdp', axis=0, tiled=True)]
    pallas_call x0 -> x1, Pallas kernels: none -> 414 us  [local_layer(): pl.pallas_call(functools.partial(kernel, (nf, nx, D, F, rows, nrb, ns)),...]
    dot_general x9 -> x0, matrix products: 325 us -> none  [the longest x1 56.2 us: local_layer(): jnp.einsum('bqhd,bkhd->bhqk', query_rot, key_all, preferred_element_type=...]
    sub x1 -> x0, other arithmetic: 99.6 us -> none  [local_layer(): jax.nn.softmax(jnp.where(allowed, scores, MASK_VALUE), axis=-1)]
    another operation x1 -> x0, other arithmetic: 36.7 us -> none
    slice x1, local copies, waits for them, and re-layouts: 34.8 us -> 0.01 us  [local_layer(): mask_t = (pos[None, :qt] <= pos[:qt, None]).astype(F32)]
    all_gather x2 -> x0, blocking collectives: 21.8 us -> none  [gather_weight(): return lax.all_gather(weight_shard, 'fsdp', axis=0, tiled=True)]
    unnamed x8 -> x1, local copies, waits for them, and re-layouts: 25 us -> 6.61 us
  transfers between devices with their start and end apart: 9 -> 0, of which waited for: 8 -> 0; matrix products, arithmetic and copies ran while one was open for 33% -> 0% of each run, Pallas kernels for 0% -> 0%
where the time goes in v1:
time: 430 us; the launch traced here: 427 us
  Pallas kernels  414 us (96%)
  local copies, waits for them, and re-layouts  8.07 us (2%)
  other arithmetic  4.7 us (1%)
    pallas_call x1, Pallas kernels, local_layer(): pl.pallas_call(functools.partial(kernel, (nf, nx, D, F, rows, nrb, ns)),...  414 us

profile of v1, /device:TPU:97, one launch (start us, length us, event | category | flops | bytes accessed | tf_op | source)
XLA Modules:
  0.0 427.1 jit_solution(16153376022888719734)
XLA Ops:
  0.0 0.1 pad.6.clone
  0.1 0.7 broadcast_in_dim.6
  0.8 0.7 broadcast_in_dim.14
  1.5 0.7 maximum_convert_fusion.gin
  2.2 0.8 compare_convert_fusion.mask_t
  3.0 1.9 fusion
  4.9 1.3 pad_maximum_fusion
  6.2 414.3 %layer.1 = (bf16[12,8,16,2048]{3,2,1,0:T(8,128)(2,1)}, bf16[8,3,3,512,256]{4,3,2,1,0:T(8,128)(2,1)}, bf16[8,1,3,512,256]{4,3,2,1,0:T(8,128)(2,1)}, bf16[22,2,3,5...) custom-call(bf16[12,8,16,2048]{3,2,1,0:T(8,128)(2,1)} %bitcast.3, f32[8,512]{1,0:T(8,128)} %maximum_convert_fusion.gin, ...), custom_call_target="tpu_custom_call" | custom-call | flops 170000007168 | bytes 400000000 | tf_op jit(solution)/shard_map/layer/pallas_call | solution.py:534
  420.5 6.6 %copy.12 = bf16[12,128,2048]{2,1,0:T(8,128)(2,1)} copy(bf16[12,128,2048]{2,1,0:T(8,128)(2,1)} %bitcast.2) | data formatting | bytes 12582912
  (5 shorter events, 0.0 us)
